TPU v7x, 256 devices: a whole 4x4x8 slice. The times are simulated.
256 devices in a mesh: grp: 16 (over z, core), row: 16 (over y, x).
Axes of the slice: x: 4, y: 4, z: 8, core: 2. Of those that a mesh axis runs over, the one named last changes fastest.
Arguments:
- theta: float32 [32, 512, 512], P('grp', 'row'), may hold values from -8 to 8
- left_env: bfloat16 [32, 8, 512, 512], P('grp', None, 'row'), may hold values from -1.5 to 1.5
- right_env: bfloat16 [32, 8, 512, 512], P('grp', None, 'row'), may hold values from -3.5 to 3.5
- lengths: int32 [32, 2], P('grp'), may hold values from 128 to 512
Outputs:
- evolved: float32 [32, 512, 512], P('grp', 'row')
- hessenberg: float32 [8, 8], replicated
All inputs are finite; a program needn't handle non-finite values.
Results may differ from a plain program's by a relative error of at most 0.0029.
Values may be sent and summed in bfloat16 or wider, within the bound.
No kernel may reach another device: no remote copies, remote signals or barrier semaphores. Data moves between devices by JAX's collectives and lax.ppermute only.
A program may use at most 64 MiB of HBM per device.

v0:
```python
import functools
import jax
import jax.numpy as jnp
from jax import lax
from jax.sharding import Mesh
from jax.sharding import PartitionSpec as P

KRYLOV = 8
ROW = ("row_0", "row_1")
GRP_ROW = ("grp_0", "grp_1", "row_0", "row_1")
GRP = ("grp_0", "grp_1")
epsilon = 1e-06
time_step = 0.5


def split_up(value, dim, length):
    dims = value.shape
    tiles = value.reshape(*dims[:dim], length, dims[dim] // length, *dims[dim + 1 :])
    return jnp.moveaxis(tiles, dim, 0)


def sent_and_summed(value, axis, dim):
    tiles = split_up(value, dim, lax.axis_size(axis))
    arrived = lax.all_to_all(tiles, axis, split_axis=0, concat_axis=0, tiled=True)
    return arrived.sum(axis=0)


def over_axes(value, axes):
    return functools.reduce(lax.psum, axes, value)


def propagate(hessenberg):
    krylov_size = hessenberg.shape[0]
    scaled = time_step * hessenberg
    series = jnp.eye(krylov_size, dtype=jnp.float32)
    series_term = jnp.eye(krylov_size, dtype=jnp.float32)
    for degree in range(1, 19):
        series_term = jnp.dot(series_term, scaled, precision=lax.Precision.HIGHEST) / degree
        series = series + series_term
    return series[:, 0]


def local(theta, left_env, right_env, lengths):
    local_rows = theta.shape[1]
    sect_width = theta.shape[2]
    row_start = lax.axis_index(ROW) * local_rows
    row_ids = row_start + lax.broadcasted_iota(jnp.int32, (1, local_rows, 1), 1)
    col_ids = lax.broadcasted_iota(jnp.int32, (1, 1, sect_width), 2)
    live_mask = (
        (row_ids < lengths[:, 0][:, None, None]) & (col_ids < lengths[:, 1][:, None, None])
    ).astype(jnp.float32)
    right_full = lax.all_gather(right_env, ROW, axis=2, tiled=True)
    start_block = theta * live_mask
    norm_zero = jnp.sqrt(over_axes(jnp.sum(start_block * start_block), GRP_ROW) + epsilon)
    krylov_basis = [start_block / norm_zero]
    krylov_size = KRYLOV
    hessenberg = jnp.zeros((krylov_size, krylov_size), jnp.float32)
    for column in range(krylov_size):
        packed = krylov_basis[column].astype(jnp.bfloat16)
        inner_terms = jnp.einsum(
            "sab,swbc->swac", packed, right_full, preferred_element_type=jnp.float32
        )
        inner_terms = inner_terms.astype(jnp.bfloat16)
        partial_image = jnp.einsum(
            "swba,swbc->sac", left_env, inner_terms, preferred_element_type=jnp.float32
        )
        image = sent_and_summed(partial_image, ROW, 1) * live_mask
        local_dots = jnp.stack([jnp.sum(vector * image) for vector in krylov_basis])
        coefficients, squared = (
            over_axes(local_dots, GRP_ROW),
            over_axes(jnp.sum(image * image), GRP_ROW),
        )
        for previous in range(column + 1):
            image = image - coefficients[previous] * krylov_basis[previous]
        hessenberg = hessenberg.at[: column + 1, column].set(coefficients)
        if column + 1 < krylov_size:
            beta_norm = jnp.sqrt(squared - jnp.sum(coefficients * coefficients) + epsilon)
            hessenberg = hessenberg.at[column + 1, column].set(beta_norm)
            krylov_basis.append(image / beta_norm)
    weights = propagate(hessenberg)
    evolved = jnp.zeros_like(start_block)
    for column in range(krylov_size):
        evolved = evolved + weights[column] * krylov_basis[column]
    return (norm_zero * evolved, hessenberg)


def solution(mesh):
    finer = Mesh(mesh.devices.reshape(8, 2, 4, 4), ("grp_0", "grp_1", "row_0", "row_1"))
    return jax.shard_map(
        local,
        mesh=finer,
        in_specs=(
            P(GRP, ROW, None),
            P(GRP, None, ROW, None),
            P(GRP, None, ROW, None),
            P(GRP, None),
        ),
        out_specs=(P(GRP, ROW, None), P()),
        check_vma=False,
    )
```

profile of v0, /device:TPU:32, one launch (start us, length us, event | category | flops | bytes accessed | tf_op | source)
XLA Modules:
  0.0 776.2 jit_solution(253862596949875197)
XLA Ops:
  10.7 18.5 %psum.448 = f32[]{:T(128)} all-reduce(f32[]{:T(128)} %multiply_reduce_fusion.43), channel_id=1, replica_groups=mesh['grp_0'=8,'grp_1'=2,'row_0'=4,'row_1'=4] {'grp_0'}, use_global_device_ids=true, to_apply=%region_1.0 | all-reduce | flops 1 | bytes 8 | tf_op jit(solution)/shard_map/psum | solution.py:29
  32.2 11.3 %psum.450 = f32[]{:T(128)} all-reduce(f32[]{:T(128)} %psum.449), channel_id=1, replica_groups=mesh['grp_0'=8,'grp_1'=2,'row_0'=4,'row_1'=4] {'row_0'}, use_global_device_ids=true, to_apply=%region_3.0 | all-reduce | flops 1 | bytes 8 | tf_op jit(solution)/shard_map/psum | solution.py:29
  43.6 11.1 %psum.451 = f32[]{:T(128)} all-reduce(f32[]{:T(128)} %psum.450), channel_id=1, replica_groups=mesh['grp_0'=8,'grp_1'=2,'row_0'=4,'row_1'=4] {'row_1'}, use_global_device_ids=true, to_apply=%region_4.0 | all-reduce | flops 1 | bytes 8 | tf_op jit(solution)/shard_map/psum | solution.py:29
  55.4 33.5 %all-gather.2.cloned.1.call-done = bf16[2,8,512,512]{3,2,1,0:T(8,128)(2,1)} async-done(((bf16[2,8,32,512]{3,2,1,0:T(8,128)(2,1)}), bf16[2,8,512,512]{3,2,1,0:T(8,128)(2,1)}) %all-gather.2.cloned.1.call-update) | async-done | bytes 8388624 | tf_op jit(solution)/shard_map/all_gather | solution.py:52
  88.9 5.4 fusion.1
  94.5 33.3 %all_to_all.40 = f32[16,2,32,512]{3,2,1,0:T(8,128)S(1)} all-to-all(f32[16,2,32,512]{3,2,1,0:T(8,128)S(1)} %bitcast.287), channel_id=1, replica_groups=mesh['grp_0'=8,'grp_1'=2,'row_0'=4,'row_1'=4] {'row_0','row_1'}, dimensions={0} | all-to-all | bytes 4194304 | tf_op jit(solution)/shard_map/all_to_all | solution.py:24
  128.7 16.7 %all-reduce.7 = (f32[]{:T(128)}, f32[1]{0:T(128)}) all-reduce(f32[]{:T(128)} %get-tuple-element.224, f32[1]{0:T(128)} %bitcast.8), channel_id=1, replica_groups=mesh['grp_0'=8,'grp_1'=2,'row_0'=4,'row_1'=4] {'grp_0'}, use_global_device_ids=true, to_apply=%region_12.0 | all-reduce | flops 2 | bytes 16 | tf_op jit(solution)/shard_map/psum | solution.py:29
  148.5 9.2 %all-reduce.21 = (f32[]{:T(128)}, f32[1]{0:T(128)}) all-reduce(f32[]{:T(128)} %get-tuple-element.281, f32[1]{0:T(128)} %get-tuple-element.282), channel_id=1, replica_groups=mesh['grp_0'=8,'grp_1'=2,'row_0'=4,'row_1'=4] {'row_0'}, use_global_device_ids=true, to_apply=%region_14.0 | all-reduce | flops 2 | bytes 16 | tf_op jit(solution)/shard_map/psum | solution.py:29
  157.6 9.2 %all-reduce.14 = (f32[]{:T(128)}, f32[1]{0:T(128)}) all-reduce(f32[]{:T(128)} %get-tuple-element.267, f32[1]{0:T(128)} %get-tuple-element.268), channel_id=1, replica_groups=mesh['grp_0'=8,'grp_1'=2,'row_0'=4,'row_1'=4] {'row_1'}, use_global_device_ids=true, to_apply=%region_15.0 | all-reduce | flops 2 | bytes 16 | tf_op jit(solution)/shard_map/psum | solution.py:29
  169.6 5.3 fusion.3
  175.1 27.9 %all_to_all.41 = f32[16,2,32,512]{3,2,1,0:T(8,128)S(1)} all-to-all(f32[16,2,32,512]{3,2,1,0:T(8,128)S(1)} %bitcast.288), channel_id=1, replica_groups=mesh['grp_0'=8,'grp_1'=2,'row_0'=4,'row_1'=4] {'row_0','row_1'}, dimensions={0} | all-to-all | bytes 4194304 | tf_op jit(solution)/shard_map/all_to_all | solution.py:24
  205.2 16.6 %all-reduce.6 = (f32[]{:T(128)}, f32[2]{0:T(128)S(1)}) all-reduce(f32[]{:T(128)} %get-tuple-element.222, f32[2]{0:T(128)S(1)} %pad_maximum_fusion), channel_id=1, replica_groups=mesh['grp_0'=8,'grp_1'=2,'row_0'=4,'row_1'=4] {'grp_0'}, use_global_device_ids=true, to_apply=%region_24.0 | all-reduce | flops 3 | bytes 24 | tf_op jit(solution)/shard_map/psum | solution.py:29
  224.9 9.2 %all-reduce.20 = (f32[]{:T(128)}, f32[2]{0:T(128)S(1)}) all-reduce(f32[]{:T(128)} %get-tuple-element.279, f32[2]{0:T(128)S(1)} %get-tuple-element.280), channel_id=1, replica_groups=mesh['grp_0'=8,'grp_1'=2,'row_0'=4,'row_1'=4] {'row_0'}, use_global_device_ids=true, to_apply=%region_26.0 | all-reduce | flops 3 | bytes 24 | tf_op jit(solution)/shard_map/psum | solution.py:29
  234.1 9.2 %all-reduce.13 = (f32[]{:T(128)}, f32[2]{0:T(128)S(1)}) all-reduce(f32[]{:T(128)} %get-tuple-element.265, f32[2]{0:T(128)S(1)} %get-tuple-element.266), channel_id=1, replica_groups=mesh['grp_0'=8,'grp_1'=2,'row_0'=4,'row_1'=4] {'row_1'}, use_global_device_ids=true, to_apply=%region_27.0 | all-reduce | flops 3 | bytes 24 | tf_op jit(solution)/shard_map/psum | solution.py:29
  247.1 5.3 fusion.5
  252.6 27.9 %all_to_all.42 = f32[16,2,32,512]{3,2,1,0:T(8,128)S(1)} all-to-all(f32[16,2,32,512]{3,2,1,0:T(8,128)S(1)} %bitcast.289), channel_id=1, replica_groups=mesh['grp_0'=8,'grp_1'=2,'row_0'=4,'row_1'=4] {'row_0','row_1'}, dimensions={0} | all-to-all | bytes 4194304 | tf_op jit(solution)/shard_map/all_to_all | solution.py:24
  283.2 15.6 %all-reduce.5 = (f32[]{:T(128)}, f32[3]{0:T(128)S(1)}) all-reduce(f32[]{:T(128)} %get-tuple-element.219, f32[3]{0:T(128)S(1)} %pad_maximum_fusion.1), channel_id=1, replica_groups=mesh['grp_0'=8,'grp_1'=2,'row_0'=4,'row_1'=4] {'grp_0'}, use_global_device_ids=true, to_apply=%region_39.0 | all-reduce | flops 4 | bytes 32 | tf_op jit(solution)/shard_map/psum | solution.py:29
  302.0 9.2 %all-reduce.19 = (f32[]{:T(128)}, f32[3]{0:T(128)S(1)}) all-reduce(f32[]{:T(128)} %get-tuple-element.277, f32[3]{0:T(128)S(1)} %get-tuple-element.278), channel_id=1, replica_groups=mesh['grp_0'=8,'grp_1'=2,'row_0'=4,'row_1'=4] {'row_0'}, use_global_device_ids=true, to_apply=%region_41.0 | all-reduce | flops 4 | bytes 32 | tf_op jit(solution)/shard_map/psum | solution.py:29
  311.2 9.2 %all-reduce.12 = (f32[]{:T(128)}, f32[3]{0:T(128)S(1)}) all-reduce(f32[]{:T(128)} %get-tuple-element.263, f32[3]{0:T(128)S(1)} %get-tuple-element.264), channel_id=1, replica_groups=mesh['grp_0'=8,'grp_1'=2,'row_0'=4,'row_1'=4] {'row_1'}, use_global_device_ids=true, to_apply=%region_42.0 | all-reduce | flops 4 | bytes 32 | tf_op jit(solution)/shard_map/psum | solution.py:29
  324.8 5.3 fusion.7
  330.3 27.9 %all_to_all.43 = f32[16,2,32,512]{3,2,1,0:T(8,128)S(1)} all-to-all(f32[16,2,32,512]{3,2,1,0:T(8,128)S(1)} %bitcast.290), channel_id=1, replica_groups=mesh['grp_0'=8,'grp_1'=2,'row_0'=4,'row_1'=4] {'row_0','row_1'}, dimensions={0} | all-to-all | bytes 4194304 | tf_op jit(solution)/shard_map/all_to_all | solution.py:24
  361.6 15.9 %all-reduce.4 = (f32[]{:T(128)}, f32[4]{0:T(128)S(1)}) all-reduce(f32[]{:T(128)} %get-tuple-element.215, f32[4]{0:T(128)S(1)} %pad_maximum_fusion.2), channel_id=1, replica_groups=mesh['grp_0'=8,'grp_1'=2,'row_0'=4,'row_1'=4] {'grp_0'}, use_global_device_ids=true, to_apply=%region_55.0 | all-reduce | flops 5 | bytes 40 | tf_op jit(solution)/shard_map/psum | solution.py:29
  380.6 9.2 %all-reduce.18 = (f32[]{:T(128)}, f32[4]{0:T(128)S(1)}) all-reduce(f32[]{:T(128)} %get-tuple-element.275, f32[4]{0:T(128)S(1)} %get-tuple-element.276), channel_id=1, replica_groups=mesh['grp_0'=8,'grp_1'=2,'row_0'=4,'row_1'=4] {'row_0'}, use_global_device_ids=true, to_apply=%region_57.0 | all-reduce | flops 5 | bytes 40 | tf_op jit(solution)/shard_map/psum | solution.py:29
  389.7 9.4 %all-reduce.11 = (f32[]{:T(128)}, f32[4]{0:T(128)S(1)}) all-reduce(f32[]{:T(128)} %get-tuple-element.261, f32[4]{0:T(128)S(1)} %get-tuple-element.262), channel_id=1, replica_groups=mesh['grp_0'=8,'grp_1'=2,'row_0'=4,'row_1'=4] {'row_1'}, use_global_device_ids=true, to_apply=%region_58.0 | all-reduce | flops 5 | bytes 40 | tf_op jit(solution)/shard_map/psum | solution.py:29
  404.1 5.3 fusion.9
  409.6 27.9 %all_to_all.44 = f32[16,2,32,512]{3,2,1,0:T(8,128)S(1)} all-to-all(f32[16,2,32,512]{3,2,1,0:T(8,128)S(1)} %bitcast.291), channel_id=1, replica_groups=mesh['grp_0'=8,'grp_1'=2,'row_0'=4,'row_1'=4] {'row_0','row_1'}, dimensions={0} | all-to-all | bytes 4194304 | tf_op jit(solution)/shard_map/all_to_all | solution.py:24
  441.4 15.7 %all-reduce.3 = (f32[]{:T(128)}, f32[5]{0:T(128)S(1)}) all-reduce(f32[]{:T(128)} %get-tuple-element.209, f32[5]{0:T(128)S(1)} %stack.147), channel_id=1, replica_groups=mesh['grp_0'=8,'grp_1'=2,'row_0'=4,'row_1'=4] {'grp_0'}, use_global_device_ids=true, to_apply=%region_72.0 | all-reduce | flops 6 | bytes 48 | tf_op jit(solution)/shard_map/psum | solution.py:29
  460.1 9.2 %all-reduce.17 = (f32[]{:T(128)}, f32[5]{0:T(128)S(1)}) all-reduce(f32[]{:T(128)} %get-tuple-element.273, f32[5]{0:T(128)S(1)} %get-tuple-element.274), channel_id=1, replica_groups=mesh['grp_0'=8,'grp_1'=2,'row_0'=4,'row_1'=4] {'row_0'}, use_global_device_ids=true, to_apply=%region_74.0 | all-reduce | flops 6 | bytes 48 | tf_op jit(solution)/shard_map/psum | solution.py:29
  469.3 9.2 %all-reduce.10 = (f32[]{:T(128)}, f32[5]{0:T(128)S(1)}) all-reduce(f32[]{:T(128)} %get-tuple-element.259, f32[5]{0:T(128)S(1)} %get-tuple-element.260), channel_id=1, replica_groups=mesh['grp_0'=8,'grp_1'=2,'row_0'=4,'row_1'=4] {'row_1'}, use_global_device_ids=true, to_apply=%region_75.0 | all-reduce | flops 6 | bytes 48 | tf_op jit(solution)/shard_map/psum | solution.py:29
  484.2 5.2 fusion.11
  489.7 27.9 %all_to_all.45 = f32[16,2,32,512]{3,2,1,0:T(8,128)S(1)} all-to-all(f32[16,2,32,512]{3,2,1,0:T(8,128)S(1)} %bitcast.292), channel_id=1, replica_groups=mesh['grp_0'=8,'grp_1'=2,'row_0'=4,'row_1'=4] {'row_0','row_1'}, dimensions={0} | all-to-all | bytes 4194304 | tf_op jit(solution)/shard_map/all_to_all | solution.py:24
  522.4 15.9 %all-reduce.2 = (f32[]{:T(128)}, f32[6]{0:T(128)S(1)}) all-reduce(f32[]{:T(128)} %get-tuple-element.203, f32[6]{0:T(128)S(1)} %stack.154), channel_id=1, replica_groups=mesh['grp_0'=8,'grp_1'=2,'row_0'=4,'row_1'=4] {'grp_0'}, use_global_device_ids=true, to_apply=%region_90.0 | all-reduce | flops 7 | bytes 56 | tf_op jit(solution)/shard_map/psum | solution.py:29
  541.4 9.2 %all-reduce.16 = (f32[]{:T(128)}, f32[6]{0:T(128)S(1)}) all-reduce(f32[]{:T(128)} %get-tuple-element.271, f32[6]{0:T(128)S(1)} %get-tuple-element.272), channel_id=1, replica_groups=mesh['grp_0'=8,'grp_1'=2,'row_0'=4,'row_1'=4] {'row_0'}, use_global_device_ids=true, to_apply=%region_92.0 | all-reduce | flops 7 | bytes 56 | tf_op jit(solution)/shard_map/psum | solution.py:29
  550.5 9.2 %all-reduce.9 = (f32[]{:T(128)}, f32[6]{0:T(128)S(1)}) all-reduce(f32[]{:T(128)} %get-tuple-element.257, f32[6]{0:T(128)S(1)} %get-tuple-element.258), channel_id=1, replica_groups=mesh['grp_0'=8,'grp_1'=2,'row_0'=4,'row_1'=4] {'row_1'}, use_global_device_ids=true, to_apply=%region_93.0 | all-reduce | flops 7 | bytes 56 | tf_op jit(solution)/shard_map/psum | solution.py:29
  565.9 5.3 fusion.13
  579.3 24.5 %all-to-all-done.6 = f32[16,2,32,512]{3,2,1,0:T(8,128)S(1)} async-done(((f32[16,2,32,512]{3,2,1,0:T(8,128)}), f32[16,2,32,512]{3,2,1,0:T(8,128)S(1)}, u32[]{:S(2)}, u32[]{:S(2)}) %all-to-all-start.6) | async-done | bytes 2097184 | tf_op jit(solution)/shard_map/all_to_all | solution.py:24
  606.4 4.4 stack.162
  610.7 15.7 %all-reduce.1 = (f32[]{:T(128)}, f32[7]{0:T(128)S(1)}) all-reduce(f32[]{:T(128)} %get-tuple-element.196, f32[7]{0:T(128)S(1)} %stack.162), channel_id=1, replica_groups=mesh['grp_0'=8,'grp_1'=2,'row_0'=4,'row_1'=4] {'grp_0'}, use_global_device_ids=true, to_apply=%region_109.0 | all-reduce | flops 8 | bytes 64 | tf_op jit(solution)/shard_map/psum | solution.py:29
  629.5 8.6 %all-reduce.15 = (f32[]{:T(128)}, f32[7]{0:T(128)S(1)}) all-reduce(f32[]{:T(128)} %get-tuple-element.269, f32[7]{0:T(128)S(1)} %get-tuple-element.270), channel_id=1, replica_groups=mesh['grp_0'=8,'grp_1'=2,'row_0'=4,'row_1'=4] {'row_0'}, use_global_device_ids=true, to_apply=%region_111.0 | all-reduce | flops 8 | bytes 64 | tf_op jit(solution)/shard_map/psum | solution.py:29
  638.1 8.9 %all-reduce.8 = (f32[]{:T(128)}, f32[7]{0:T(128)S(1)}) all-reduce(f32[]{:T(128)} %get-tuple-element.255, f32[7]{0:T(128)S(1)} %get-tuple-element.256), channel_id=1, replica_groups=mesh['grp_0'=8,'grp_1'=2,'row_0'=4,'row_1'=4] {'row_1'}, use_global_device_ids=true, to_apply=%region_112.0 | all-reduce | flops 8 | bytes 64 | tf_op jit(solution)/shard_map/psum | solution.py:29
  649.6 6.0 subtract_divide_fusion
  655.6 5.3 fusion.15
  662.5 4.0 all-to-all-start.7
  711.8 5.1 stack.171
  717.0 15.3 %psum.508 = f32[8]{0:T(128)S(1)} all-reduce(f32[8]{0:T(128)S(1)} %stack.171), channel_id=1, replica_groups=mesh['grp_0'=8,'grp_1'=2,'row_0'=4,'row_1'=4] {'grp_0'}, use_global_device_ids=true, to_apply=%region_123.0 | all-reduce | flops 8 | bytes 64 | tf_op jit(solution)/shard_map/psum | solution.py:29
  738.0 10.9 %psum.510 = f32[8]{0:T(128)S(1)} all-reduce(f32[8]{0:T(128)S(1)} %psum.509), channel_id=1, replica_groups=mesh['grp_0'=8,'grp_1'=2,'row_0'=4,'row_1'=4] {'row_0'}, use_global_device_ids=true, to_apply=%region_125.0 | all-reduce | flops 8 | bytes 64 | tf_op jit(solution)/shard_map/psum | solution.py:29
  749.0 10.4 %psum.511 = f32[8,1]{1,0:T(8,128)S(1)} all-reduce(f32[8,1]{1,0:T(8,128)S(1)} %copy.27), channel_id=1, replica_groups=mesh['grp_0'=8,'grp_1'=2,'row_0'=4,'row_1'=4] {'row_1'}, use_global_device_ids=true, to_apply=%region_126.0 | all-reduce | flops 8 | bytes 64 | tf_op jit(solution)/shard_map/psum | solution.py:29
  762.7 6.7 add_multiply_fusion
  (144 shorter events, 134.9 us)
Async XLA Ops:
  7.2 81.7 %copy-start = (bf16[2,8,32,512]{3,2,1,0:T(8,128)(2,1)S(1)}, bf16[2,8,32,512]{3,2,1,0:T(8,128)(2,1)}, u32[]{:S(2)}) copy-start(bf16[2,8,32,512]{3,2,1,0:T(8,128)(2,1)} %param.35) | copy-start | bytes 1572868
  7.2 81.7 %all-gather.2.cloned.1.call-start = ((), (), s32[]{:S(2)}) async-start(), calls=%async_computation.8 | async-start | bytes 8912896 | tf_op jit(solution)/shard_map/all_gather | solution.py:52
  55.4 72.6 %copy-start.1 = (f32[2,32,512]{2,1,0:T(8,128)S(1)}, f32[2,32,512]{2,1,0:T(8,128)}, u32[]{:S(2)}) copy-start(f32[2,32,512]{2,1,0:T(8,128)} %param.34) | copy-start | bytes 393220
  243.3 2.5 copy-start.7
  320.4 2.5 copy-start.6
  399.1 2.4 copy-start.5
  478.5 39.0 %copy-start.4 = (f32[5]{0:T(128)}, f32[5]{0:T(128)S(1)}, u32[]{:S(2)}) copy-start(f32[5]{0:T(128)S(1)} %get-tuple-element.246) | copy-start | bytes 64
  559.8 13.0 %copy-start.3 = (f32[6]{0:T(128)}, f32[6]{0:T(128)S(1)}, u32[]{:S(2)}) copy-start(f32[6]{0:T(128)S(1)} %get-tuple-element.244) | copy-start | bytes 76
  572.8 31.0 %all-to-all-start.6 = ((f32[16,2,32,512]{3,2,1,0:T(8,128)}), f32[16,2,32,512]{3,2,1,0:T(8,128)S(1)}, u32[]{:S(2)}, u32[]{:S(2)}) async-start(f32[16,2,32,512]{3,2,1,0:T(8,128)} %bitcast.286), calls=%async_computation.6 | async-start | bytes 4194304 | tf_op jit(solution)/shard_map/all_to_all | solution.py:24
  662.5 46.6 %all-to-all-start.7 = ((f32[16,2,32,512]{3,2,1,0:T(8,128)}), f32[16,2,32,512]{3,2,1,0:T(8,128)S(1)}, u32[]{:S(2)}, u32[]{:S(2)}) async-start(f32[16,2,32,512]{3,2,1,0:T(8,128)} %bitcast.285), calls=%async_computation.7 | async-start | bytes 4194304 | tf_op jit(solution)/shard_map/all_to_all | solution.py:24
  759.6 9.8 %copy-start.2 = (f32[8,8]{1,0:T(8,128)}, f32[8,8]{1,0:T(8,128)S(1)}, u32[]{:S(2)}) copy-start(f32[8,8]{1,0:T(8,128)S(1)} %scatter.74) | copy-start | bytes 772
Sparse Core Ops, SparseCore 0:
  10.4 78.4 all-gather.1
where the time goes:
time: 779 us; the launch traced here: 776 us
  blocking collectives  517 us (66%)
  other arithmetic  70.9 us (9%)
  waiting for transfers between devices  58.6 us (8%)
  local copies, waits for them, and re-layouts  52.1 us (7%)
  matrix products  44.7 us (6%)
  between operations  24.8 us (3%)
    psum x36, blocking collectives, over_axes(): return functools.reduce(lax.psum, axes, value)  345 us
    all_to_all x6, blocking collectives, sent_and_summed(): lax.all_to_all(tiles, axis, split_axis=0, concat_axis=0, tiled=True)  173 us
    dot_general x8, matrix products, local(): jnp.einsum('swba,swbc->sac', left_env, inner_terms, preferred_element_typ...  42.2 us
    all_gather x1, waiting for transfers between devices, local(): right_full = lax.all_gather(right_env, ROW, axis=2, tiled=True)  33.5 us
    all_to_all x2, waiting for transfers between devices, sent_and_summed(): lax.all_to_all(tiles, axis, split_axis=0, concat_axis=0, tiled=True)  24.5 us
    another operation x15, other arithmetic  23.1 us
    div x7, other arithmetic, local(): krylov_basis.append(image / beta_norm)  19.2 us
    another operation x4, local copies, waits for them, and re-layouts, local(): local_dots = jnp.stack([jnp.sum(vector * image) for vector in krylov_basis])  16.3 us
  transfers between devices with their start and end apart: 3, of which 2 were waited for; matrix products, arithmetic and copies ran while one was open for 6% of the time, Pallas kernels for 0%

commit v1 on v0

--- a/solution.py
+++ b/solution.py
@@ -49,7 +49,9 @@
     live_mask = (
         (row_ids < lengths[:, 0][:, None, None]) & (col_ids < lengths[:, 1][:, None, None])
     ).astype(jnp.float32)
-    right_full = lax.all_gather(right_env, ROW, axis=2, tiled=True)
+    right_full = jnp.concatenate(
+        lax.all_to_all(jnp.stack([right_env] * lax.axis_size(ROW)), ROW, 0, 0), axis=2
+    )
     start_block = theta * live_mask
     norm_zero = jnp.sqrt(over_axes(jnp.sum(start_block * start_block), GRP_ROW) + epsilon)
     krylov_basis = [start_block / norm_zero]

time: 779 us -> 833 us (1.069)
  blocking collectives: 517 us -> 599 us
  waiting for transfers between devices: 58.6 us -> 25 us
  between operations: 24.8 us -> 11.4 us
  local copies, waits for them, and re-layouts: 52.1 us -> 64.2 us
    psum x36, blocking collectives: 345 us -> 428 us  [over_axes(): return functools.reduce(lax.psum, axes, value)]
    all_gather x1 -> x0, waiting for transfers between devices: 33.5 us -> none  [local(): right_full = lax.all_gather(right_env, ROW, axis=2, tiled=True)]
    another operation x14 -> x15, local copies, waits for them, and re-layouts: 12.3 us -> 16.9 us
  transfers between devices with their start and end apart: 3 -> 3, of which waited for: 2 -> 1; matrix products, arithmetic and copies ran while one was open for 6% -> 5% of each run, Pallas kernels for 0% -> 0%
where the time goes in v1:
time: 833 us; the launch traced here: 830 us
  blocking collectives  599 us (72%)
  other arithmetic  70.4 us (8%)
  local copies, waits for them, and re-layouts  64.2 us (8%)
  matrix products  44.7 us (5%)
  waiting for transfers between devices  25 us (3%)
  starting transfers between devices  14.9 us (2%)
  between operations  11.4 us (1%)
    psum x36, blocking collectives, over_axes(): return functools.reduce(lax.psum, axes, value)  428 us
    all_to_all x6, blocking collectives, sent_and_summed(): lax.all_to_all(tiles, axis, split_axis=0, concat_axis=0, tiled=True)  171 us
    dot_general x8, matrix products, local(): jnp.einsum('swba,swbc->sac', left_env, inner_terms, preferred_element_typ...  42.2 us
    all_to_all x2, waiting for transfers between devices, sent_and_summed(): lax.all_to_all(tiles, axis, split_axis=0, concat_axis=0, tiled=True)  25 us
    another operation x15, other arithmetic  22.6 us
    div x7, other arithmetic, local(): krylov_basis.append(image / beta_norm)  20.2 us
  transfers between devices with their start and end apart: 3, of which 1 were waited for; matrix products, arithmetic and copies ran while one was open for 5% of the time, Pallas kernels for 0%

profile of v1, /device:TPU:32, one launch (start us, length us, event | category | flops | bytes accessed | tf_op | source)
XLA Modules:
  0.0 829.6 jit_solution(14678832597537749762)
XLA Ops:
  0.6 5.4 stack.148
  6.0 7.2 all-to-all-start
  14.3 18.5 %psum.448 = f32[]{:T(128)} all-reduce(f32[]{:T(128)} %multiply_reduce_fusion.43), channel_id=1, replica_groups=mesh['grp_0'=8,'grp_1'=2,'row_0'=4,'row_1'=4] {'grp_0'}, use_global_device_ids=true, to_apply=%region_1.0 | all-reduce | flops 1 | bytes 8 | tf_op jit(solution)/shard_map/psum | solution.py:29
  35.9 44.1 %psum.450 = f32[]{:T(128)} all-reduce(f32[]{:T(128)} %psum.449), channel_id=1, replica_groups=mesh['grp_0'=8,'grp_1'=2,'row_0'=4,'row_1'=4] {'row_0'}, use_global_device_ids=true, to_apply=%region_3.0 | all-reduce | flops 1 | bytes 8 | tf_op jit(solution)/shard_map/psum | solution.py:29
  80.0 59.5 %psum.451 = f32[]{:T(128)} all-reduce(f32[]{:T(128)} %psum.450), channel_id=1, replica_groups=mesh['grp_0'=8,'grp_1'=2,'row_0'=4,'row_1'=4] {'row_1'}, use_global_device_ids=true, to_apply=%region_4.0 | all-reduce | flops 1 | bytes 8 | tf_op jit(solution)/shard_map/psum | solution.py:29
  140.2 8.3 copy.20
  148.5 5.3 fusion.1
  154.0 31.6 %all_to_all.45 = f32[16,2,32,512]{3,2,1,0:T(8,128)S(1)} all-to-all(f32[16,2,32,512]{3,2,1,0:T(8,128)S(1)} %bitcast.298), channel_id=1, replica_groups=mesh['grp_0'=8,'grp_1'=2,'row_0'=4,'row_1'=4] {'row_0','row_1'}, dimensions={0} | all-to-all | bytes 4194304 | tf_op jit(solution)/shard_map/all_to_all | solution.py:24
  186.5 18.5 %all-reduce.7 = (f32[]{:T(128)}, f32[1]{0:T(128)}) all-reduce(f32[]{:T(128)} %get-tuple-element.224, f32[1]{0:T(128)} %bitcast.10), channel_id=1, replica_groups=mesh['grp_0'=8,'grp_1'=2,'row_0'=4,'row_1'=4] {'grp_0'}, use_global_device_ids=true, to_apply=%region_12.0 | all-reduce | flops 2 | bytes 16 | tf_op jit(solution)/shard_map/psum | solution.py:29
  208.1 9.2 %all-reduce.21 = (f32[]{:T(128)}, f32[1]{0:T(128)}) all-reduce(f32[]{:T(128)} %get-tuple-element.281, f32[1]{0:T(128)} %get-tuple-element.282), channel_id=1, replica_groups=mesh['grp_0'=8,'grp_1'=2,'row_0'=4,'row_1'=4] {'row_0'}, use_global_device_ids=true, to_apply=%region_14.0 | all-reduce | flops 2 | bytes 16 | tf_op jit(solution)/shard_map/psum | solution.py:29
  217.2 9.2 %all-reduce.14 = (f32[]{:T(128)}, f32[1]{0:T(128)}) all-reduce(f32[]{:T(128)} %get-tuple-element.267, f32[1]{0:T(128)} %get-tuple-element.268), channel_id=1, replica_groups=mesh['grp_0'=8,'grp_1'=2,'row_0'=4,'row_1'=4] {'row_1'}, use_global_device_ids=true, to_apply=%region_15.0 | all-reduce | flops 2 | bytes 16 | tf_op jit(solution)/shard_map/psum | solution.py:29
  229.2 5.3 fusion.3
  234.7 27.9 %all_to_all.46 = f32[16,2,32,512]{3,2,1,0:T(8,128)S(1)} all-to-all(f32[16,2,32,512]{3,2,1,0:T(8,128)S(1)} %bitcast.299), channel_id=1, replica_groups=mesh['grp_0'=8,'grp_1'=2,'row_0'=4,'row_1'=4] {'row_0','row_1'}, dimensions={0} | all-to-all | bytes 4194304 | tf_op jit(solution)/shard_map/all_to_all | solution.py:24
  264.8 17.0 %all-reduce.6 = (f32[]{:T(128)}, f32[2]{0:T(128)S(1)}) all-reduce(f32[]{:T(128)} %get-tuple-element.222, f32[2]{0:T(128)S(1)} %pad_maximum_fusion), channel_id=1, replica_groups=mesh['grp_0'=8,'grp_1'=2,'row_0'=4,'row_1'=4] {'grp_0'}, use_global_device_ids=true, to_apply=%region_24.0 | all-reduce | flops 3 | bytes 24 | tf_op jit(solution)/shard_map/psum | solution.py:29
  284.8 9.2 %all-reduce.20 = (f32[]{:T(128)}, f32[2]{0:T(128)S(1)}) all-reduce(f32[]{:T(128)} %get-tuple-element.279, f32[2]{0:T(128)S(1)} %get-tuple-element.280), channel_id=1, replica_groups=mesh['grp_0'=8,'grp_1'=2,'row_0'=4,'row_1'=4] {'row_0'}, use_global_device_ids=true, to_apply=%region_26.0 | all-reduce | flops 3 | bytes 24 | tf_op jit(solution)/shard_map/psum | solution.py:29
  294.0 9.2 %all-reduce.13 = (f32[]{:T(128)}, f32[2]{0:T(128)S(1)}) all-reduce(f32[]{:T(128)} %get-tuple-element.265, f32[2]{0:T(128)S(1)} %get-tuple-element.266), channel_id=1, replica_groups=mesh['grp_0'=8,'grp_1'=2,'row_0'=4,'row_1'=4] {'row_1'}, use_global_device_ids=true, to_apply=%region_27.0 | all-reduce | flops 3 | bytes 24 | tf_op jit(solution)/shard_map/psum | solution.py:29
  307.0 5.3 fusion.5
  312.5 27.9 %all_to_all.47 = f32[16,2,32,512]{3,2,1,0:T(8,128)S(1)} all-to-all(f32[16,2,32,512]{3,2,1,0:T(8,128)S(1)} %bitcast.300), channel_id=1, replica_groups=mesh['grp_0'=8,'grp_1'=2,'row_0'=4,'row_1'=4] {'row_0','row_1'}, dimensions={0} | all-to-all | bytes 4194304 | tf_op jit(solution)/shard_map/all_to_all | solution.py:24
  343.2 14.8 %all-reduce.5 = (f32[]{:T(128)}, f32[3]{0:T(128)S(1)}) all-reduce(f32[]{:T(128)} %get-tuple-element.219, f32[3]{0:T(128)S(1)} %pad_maximum_fusion.1), channel_id=1, replica_groups=mesh['grp_0'=8,'grp_1'=2,'row_0'=4,'row_1'=4] {'grp_0'}, use_global_device_ids=true, to_apply=%region_39.0 | all-reduce | flops 4 | bytes 32 | tf_op jit(solution)/shard_map/psum | solution.py:29
  361.1 9.2 %all-reduce.19 = (f32[]{:T(128)}, f32[3]{0:T(128)S(1)}) all-reduce(f32[]{:T(128)} %get-tuple-element.277, f32[3]{0:T(128)S(1)} %get-tuple-element.278), channel_id=1, replica_groups=mesh['grp_0'=8,'grp_1'=2,'row_0'=4,'row_1'=4] {'row_0'}, use_global_device_ids=true, to_apply=%region_41.0 | all-reduce | flops 4 | bytes 32 | tf_op jit(solution)/shard_map/psum | solution.py:29
  370.3 9.2 %all-reduce.12 = (f32[]{:T(128)}, f32[3]{0:T(128)S(1)}) all-reduce(f32[]{:T(128)} %get-tuple-element.263, f32[3]{0:T(128)S(1)} %get-tuple-element.264), channel_id=1, replica_groups=mesh['grp_0'=8,'grp_1'=2,'row_0'=4,'row_1'=4] {'row_1'}, use_global_device_ids=true, to_apply=%region_42.0 | all-reduce | flops 4 | bytes 32 | tf_op jit(solution)/shard_map/psum | solution.py:29
  383.9 5.3 fusion.7
  389.4 27.9 %all_to_all.48 = f32[16,2,32,512]{3,2,1,0:T(8,128)S(1)} all-to-all(f32[16,2,32,512]{3,2,1,0:T(8,128)S(1)} %bitcast.301), channel_id=1, replica_groups=mesh['grp_0'=8,'grp_1'=2,'row_0'=4,'row_1'=4] {'row_0','row_1'}, dimensions={0} | all-to-all | bytes 4194304 | tf_op jit(solution)/shard_map/all_to_all | solution.py:24
  420.7 16.8 %all-reduce.4 = (f32[]{:T(128)}, f32[4]{0:T(128)S(1)}) all-reduce(f32[]{:T(128)} %get-tuple-element.215, f32[4]{0:T(128)S(1)} %pad_maximum_fusion.2), channel_id=1, replica_groups=mesh['grp_0'=8,'grp_1'=2,'row_0'=4,'row_1'=4] {'grp_0'}, use_global_device_ids=true, to_apply=%region_55.0 | all-reduce | flops 5 | bytes 40 | tf_op jit(solution)/shard_map/psum | solution.py:29
  440.5 9.4 %all-reduce.18 = (f32[]{:T(128)}, f32[4]{0:T(128)S(1)}) all-reduce(f32[]{:T(128)} %get-tuple-element.275, f32[4]{0:T(128)S(1)} %get-tuple-element.276), channel_id=1, replica_groups=mesh['grp_0'=8,'grp_1'=2,'row_0'=4,'row_1'=4] {'row_0'}, use_global_device_ids=true, to_apply=%region_57.0 | all-reduce | flops 5 | bytes 40 | tf_op jit(solution)/shard_map/psum | solution.py:29
  449.9 9.2 %all-reduce.11 = (f32[]{:T(128)}, f32[4]{0:T(128)S(1)}) all-reduce(f32[]{:T(128)} %get-tuple-element.261, f32[4]{0:T(128)S(1)} %get-tuple-element.262), channel_id=1, replica_groups=mesh['grp_0'=8,'grp_1'=2,'row_0'=4,'row_1'=4] {'row_1'}, use_global_device_ids=true, to_apply=%region_58.0 | all-reduce | flops 5 | bytes 40 | tf_op jit(solution)/shard_map/psum | solution.py:29
  464.0 5.3 fusion.9
  469.5 27.9 %all_to_all.49 = f32[16,2,32,512]{3,2,1,0:T(8,128)S(1)} all-to-all(f32[16,2,32,512]{3,2,1,0:T(8,128)S(1)} %bitcast.302), channel_id=1, replica_groups=mesh['grp_0'=8,'grp_1'=2,'row_0'=4,'row_1'=4] {'row_0','row_1'}, dimensions={0} | all-to-all | bytes 4194304 | tf_op jit(solution)/shard_map/all_to_all | solution.py:24
  501.4 14.8 %all-reduce.3 = (f32[]{:T(128)}, f32[5]{0:T(128)S(1)}) all-reduce(f32[]{:T(128)} %get-tuple-element.209, f32[5]{0:T(128)S(1)} %stack.167), channel_id=1, replica_groups=mesh['grp_0'=8,'grp_1'=2,'row_0'=4,'row_1'=4] {'grp_0'}, use_global_device_ids=true, to_apply=%region_72.0 | all-reduce | flops 6 | bytes 48 | tf_op jit(solution)/shard_map/psum | solution.py:29
  519.2 9.2 %all-reduce.17 = (f32[]{:T(128)}, f32[5]{0:T(128)S(1)}) all-reduce(f32[]{:T(128)} %get-tuple-element.273, f32[5]{0:T(128)S(1)} %get-tuple-element.274), channel_id=1, replica_groups=mesh['grp_0'=8,'grp_1'=2,'row_0'=4,'row_1'=4] {'row_0'}, use_global_device_ids=true, to_apply=%region_74.0 | all-reduce | flops 6 | bytes 48 | tf_op jit(solution)/shard_map/psum | solution.py:29
  528.4 9.2 %all-reduce.10 = (f32[]{:T(128)}, f32[5]{0:T(128)S(1)}) all-reduce(f32[]{:T(128)} %get-tuple-element.259, f32[5]{0:T(128)S(1)} %get-tuple-element.260), channel_id=1, replica_groups=mesh['grp_0'=8,'grp_1'=2,'row_0'=4,'row_1'=4] {'row_1'}, use_global_device_ids=true, to_apply=%region_75.0 | all-reduce | flops 6 | bytes 48 | tf_op jit(solution)/shard_map/psum | solution.py:29
  543.3 5.2 fusion.11
  548.8 27.9 %all_to_all.50 = f32[16,2,32,512]{3,2,1,0:T(8,128)S(1)} all-to-all(f32[16,2,32,512]{3,2,1,0:T(8,128)S(1)} %bitcast.303), channel_id=1, replica_groups=mesh['grp_0'=8,'grp_1'=2,'row_0'=4,'row_1'=4] {'row_0','row_1'}, dimensions={0} | all-to-all | bytes 4194304 | tf_op jit(solution)/shard_map/all_to_all | solution.py:24
  581.4 16.8 %all-reduce.2 = (f32[]{:T(128)}, f32[6]{0:T(128)S(1)}) all-reduce(f32[]{:T(128)} %get-tuple-element.203, f32[6]{0:T(128)S(1)} %stack.174), channel_id=1, replica_groups=mesh['grp_0'=8,'grp_1'=2,'row_0'=4,'row_1'=4] {'grp_0'}, use_global_device_ids=true, to_apply=%region_90.0 | all-reduce | flops 7 | bytes 56 | tf_op jit(solution)/shard_map/psum | solution.py:29
  601.3 9.2 %all-reduce.16 = (f32[]{:T(128)}, f32[6]{0:T(128)S(1)}) all-reduce(f32[]{:T(128)} %get-tuple-element.271, f32[6]{0:T(128)S(1)} %get-tuple-element.272), channel_id=1, replica_groups=mesh['grp_0'=8,'grp_1'=2,'row_0'=4,'row_1'=4] {'row_0'}, use_global_device_ids=true, to_apply=%region_92.0 | all-reduce | flops 7 | bytes 56 | tf_op jit(solution)/shard_map/psum | solution.py:29
  610.5 9.2 %all-reduce.9 = (f32[]{:T(128)}, f32[6]{0:T(128)S(1)}) all-reduce(f32[]{:T(128)} %get-tuple-element.257, f32[6]{0:T(128)S(1)} %get-tuple-element.258), channel_id=1, replica_groups=mesh['grp_0'=8,'grp_1'=2,'row_0'=4,'row_1'=4] {'row_1'}, use_global_device_ids=true, to_apply=%region_93.0 | all-reduce | flops 7 | bytes 56 | tf_op jit(solution)/shard_map/psum | solution.py:29
  626.9 5.3 fusion.13
  639.8 25.0 %all-to-all-done.7 = f32[16,2,32,512]{3,2,1,0:T(8,128)S(1)} async-done(((f32[16,2,32,512]{3,2,1,0:T(8,128)}), f32[16,2,32,512]{3,2,1,0:T(8,128)S(1)}, u32[]{:S(2)}, u32[]{:S(2)}) %all-to-all-start.7) | async-done | bytes 2097184 | tf_op jit(solution)/shard_map/all_to_all | solution.py:24
  671.8 14.8 %all-reduce.1 = (f32[]{:T(128)}, f32[7]{0:T(128)S(1)}) all-reduce(f32[]{:T(128)} %get-tuple-element.196, f32[7]{0:T(128)S(1)} %stack.182), channel_id=1, replica_groups=mesh['grp_0'=8,'grp_1'=2,'row_0'=4,'row_1'=4] {'grp_0'}, use_global_device_ids=true, to_apply=%region_109.0 | all-reduce | flops 8 | bytes 64 | tf_op jit(solution)/shard_map/psum | solution.py:29
  689.6 8.6 %all-reduce.15 = (f32[]{:T(128)}, f32[7]{0:T(128)S(1)}) all-reduce(f32[]{:T(128)} %get-tuple-element.269, f32[7]{0:T(128)S(1)} %get-tuple-element.270), channel_id=1, replica_groups=mesh['grp_0'=8,'grp_1'=2,'row_0'=4,'row_1'=4] {'row_0'}, use_global_device_ids=true, to_apply=%region_111.0 | all-reduce | flops 8 | bytes 64 | tf_op jit(solution)/shard_map/psum | solution.py:29
  698.2 9.0 %all-reduce.8 = (f32[]{:T(128)}, f32[7]{0:T(128)S(1)}) all-reduce(f32[]{:T(128)} %get-tuple-element.255, f32[7]{0:T(128)S(1)} %get-tuple-element.256), channel_id=1, replica_groups=mesh['grp_0'=8,'grp_1'=2,'row_0'=4,'row_1'=4] {'row_1'}, use_global_device_ids=true, to_apply=%region_112.0 | all-reduce | flops 8 | bytes 64 | tf_op jit(solution)/shard_map/psum | solution.py:29
  709.8 6.0 subtract_divide_fusion
  715.8 5.3 fusion.15
  771.1 5.0 stack.191
  776.3 16.1 %psum.508 = f32[8]{0:T(128)S(1)} all-reduce(f32[8]{0:T(128)S(1)} %stack.191), channel_id=1, replica_groups=mesh['grp_0'=8,'grp_1'=2,'row_0'=4,'row_1'=4] {'grp_0'}, use_global_device_ids=true, to_apply=%region_123.0 | all-reduce | flops 8 | bytes 64 | tf_op jit(solution)/shard_map/psum | solution.py:29
  798.2 10.9 %psum.510 = f32[8]{0:T(128)S(1)} all-reduce(f32[8]{0:T(128)S(1)} %psum.509), channel_id=1, replica_groups=mesh['grp_0'=8,'grp_1'=2,'row_0'=4,'row_1'=4] {'row_0'}, use_global_device_ids=true, to_apply=%region_125.0 | all-reduce | flops 8 | bytes 64 | tf_op jit(solution)/shard_map/psum | solution.py:29
  809.3 10.4 %psum.511 = f32[8,1]{1,0:T(8,128)S(1)} all-reduce(f32[8,1]{1,0:T(8,128)S(1)} %copy.35), channel_id=1, replica_groups=mesh['grp_0'=8,'grp_1'=2,'row_0'=4,'row_1'=4] {'row_1'}, use_global_device_ids=true, to_apply=%region_126.0 | all-reduce | flops 8 | bytes 64 | tf_op jit(solution)/shard_map/psum | solution.py:29
  822.9 6.7 add_multiply_fusion
  (149 shorter events, 140.5 us)
Async XLA Ops:
  0.6 147.8 %copy-start = (bf16[2,8,32,512]{3,2,1,0:T(8,128)(2,1)S(1)}, bf16[2,8,32,512]{3,2,1,0:T(8,128)(2,1)}, u32[]{:S(2)}) copy-start(bf16[2,8,32,512]{3,2,1,0:T(8,128)(2,1)} %param.35) | copy-start | bytes 1572868
  6.0 7.2 copy-start.8
  6.0 7.6 copy-start.1
  6.0 134.2 %all-to-all-start = ((bf16[16,2,8,32,512]{4,3,2,1,0:T(8,128)(2,1)}), bf16[16,2,8,32,512]{4,3,2,1,0:T(8,128)(2,1)}, u32[]{:S(2)}, u32[]{:S(2)}) async-start(bf16[16,2,8,32,512]{4,3,2,1,0:T(8,128)(2,1)} %stack.148), calls=%async_computation | async-start | bytes 16777216 | tf_op jit(solution)/shard_map/all_to_all | solution.py:53
  303.2 2.5 copy-start.9
  379.5 2.5 copy-start.7
  459.1 2.4 copy-start.6
  537.6 39.0 %copy-start.5 = (f32[5]{0:T(128)}, f32[5]{0:T(128)S(1)}, u32[]{:S(2)}) copy-start(f32[5]{0:T(128)S(1)} %get-tuple-element.246) | copy-start | bytes 64
  576.8 45.4 %copy-start.3 = (f32[2,32,512]{2,1,0:T(8,128)}, f32[2,32,512]{2,1,0:T(8,128)S(1)}, u32[]{:S(2)}) copy-start(f32[2,32,512]{2,1,0:T(8,128)S(1)} %reduce_sum.559) | copy-start | bytes 393220
  619.7 14.1 %copy-start.4 = (f32[6]{0:T(128)}, f32[6]{0:T(128)S(1)}, u32[]{:S(2)}) copy-start(f32[6]{0:T(128)S(1)} %get-tuple-element.244) | copy-start | bytes 76
  633.8 31.0 %all-to-all-start.7 = ((f32[16,2,32,512]{3,2,1,0:T(8,128)}), f32[16,2,32,512]{3,2,1,0:T(8,128)S(1)}, u32[]{:S(2)}, u32[]{:S(2)}) async-start(f32[16,2,32,512]{3,2,1,0:T(8,128)} %bitcast.297), calls=%async_computation.7 | async-start | bytes 4194304 | tf_op jit(solution)/shard_map/all_to_all | solution.py:24
  722.7 45.8 %all-to-all-start.8 = ((f32[16,2,32,512]{3,2,1,0:T(8,128)}), f32[16,2,32,512]{3,2,1,0:T(8,128)S(1)}, u32[]{:S(2)}, u32[]{:S(2)}) async-start(f32[16,2,32,512]{3,2,1,0:T(8,128)} %bitcast.296), calls=%async_computation.8 | async-start | bytes 4194304 | tf_op jit(solution)/shard_map/all_to_all | solution.py:24
  819.8 9.8 %copy-start.2 = (f32[8,8]{1,0:T(8,128)}, f32[8,8]{1,0:T(8,128)S(1)}, u32[]{:S(2)}) copy-start(f32[8,8]{1,0:T(8,128)S(1)} %scatter.74) | copy-start | bytes 772
